TPU v7x, 32 devices: a whole 2x2x4 slice. The times are simulated.
32 devices in a mesh: tok: 8 (over z, x), voc: 4 (over y, core).
Axes of the slice: x: 2, y: 2, z: 4, core: 2. Of those that a mesh axis runs over, the one named last changes fastest.
Arguments:
- hidden: bfloat16 [256, 3584], P('tok'), may hold values from -700 to 700
- teacher_logits: bfloat16 [256, 20480], P(None, ('tok', 'voc')), may hold values from -300 to 300
- sampled_ids: int32 [256], P('tok'), may hold values from 0 to 20479
- loss_mask: int32 [256], P('tok'), may hold values from 0 to 1, as said below
- student_head: bfloat16 [3584, 20480], P(None, ('tok', 'voc')), may hold values from -0.3125 to 0.3125
Outputs:
- loss: float32 [], replicated
- sampled_ratio: float32 [256], P(('tok', 'voc'))
- hidden_grad: bfloat16 [256, 3584], P(('tok', 'voc'))
- head_grad: bfloat16 [3584, 20480], P(None, ('tok', 'voc'))
Inputs may be any that keep to these rules, and one draw needn't show every extreme that they name: `loss_mask`: at least one position is valid.
All inputs are finite; a program needn't handle non-finite values.
Results may differ from a plain program's by a relative error of at most 0.02.
Values may be sent and summed in bfloat16 or wider, within the bound.
A program may use at most 128 MiB of HBM per device.

v0:
```python
import jax
import jax.numpy as jnp
from jax import lax
from jax.sharding import PartitionSpec as P


def per_device(hidden, teacher_logits, sampled_ids, loss_mask, student_head):
    all_hidden, all_ids, all_mask = (
        lax.all_gather(hidden, "tok", axis=0, tiled=True),
        lax.all_gather(sampled_ids, "tok", axis=0, tiled=True),
        lax.all_gather(loss_mask, "tok", axis=0, tiled=True),
    )
    teacher = teacher_logits.astype(jnp.float32)
    student = jnp.dot(all_hidden, student_head, preferred_element_type=jnp.float32)
    devices = lax.axis_size(("tok", "voc"))
    position = lax.axis_index(("tok", "voc"))
    vocab_dev = student_head.shape[1]
    rows_all = all_hidden.shape[0]
    rows_own = rows_all // devices
    weight = all_mask.astype(jnp.float32)
    count = jnp.sum(weight)
    columns = position * vocab_dev + lax.broadcasted_iota(jnp.int32, (1, vocab_dev), 1)
    chosen = all_ids[:, None] == columns
    student_max, teacher_max = lax.pmax(
        (jnp.max(student, axis=1), jnp.max(teacher, axis=1)), ("tok", "voc")
    )
    shifted = jnp.exp(student - student_max[:, None])
    student_total, teacher_total, cross_term, student_pick, teacher_pick = lax.psum(
        (
            jnp.sum(shifted, axis=1),
            jnp.sum(jnp.exp(teacher - teacher_max[:, None]), axis=1),
            jnp.sum(shifted * (student - teacher), axis=1),
            jnp.sum(jnp.where(chosen, student, 0.0), axis=1),
            jnp.sum(jnp.where(chosen, teacher, 0.0), axis=1),
        ),
        ("tok", "voc"),
    )
    student_shift = student_max + jnp.log(student_total)
    teacher_shift = teacher_max + jnp.log(teacher_total)
    row_kl = cross_term / student_total - student_shift + teacher_shift
    ratio_all = student_pick - student_shift - (teacher_pick - teacher_shift)
    sampled_ratio = lax.dynamic_slice_in_dim(ratio_all, position * rows_own, rows_own, 0)
    student_log = student - student_shift[:, None]
    differ = student_log - (teacher - teacher_shift[:, None])
    dlogits = (weight[:, None] * jnp.exp(student_log) * (differ - row_kl[:, None])).astype(
        jnp.bfloat16
    )
    loss = jnp.sum(weight * row_kl) / count
    partial_sum = lax.psum_scatter(
        lax.dot_general(
            dlogits, student_head, (((1,), (1,)), ((), ())), preferred_element_type=jnp.float32
        ).astype(jnp.bfloat16),
        "tok",
        scatter_dimension=0,
        tiled=True,
    )
    hidden_sum = lax.psum_scatter(partial_sum, "voc", scatter_dimension=0, tiled=True).astype(
        jnp.float32
    )
    hidden_grad = hidden_sum.astype(jnp.bfloat16)
    head_grad = lax.dot_general(
        all_hidden, dlogits, (((0,), (0,)), ((), ())), preferred_element_type=jnp.float32
    ).astype(jnp.bfloat16)
    return (loss, sampled_ratio, hidden_grad, head_grad)


def solution(mesh):
    in_specs = (
        P("tok", None),
        P(None, ("tok", "voc")),
        P("tok"),
        P("tok"),
        P(None, ("tok", "voc")),
    )
    out_specs = (P(), P(("tok", "voc")), P(("tok", "voc"), None), P(None, ("tok", "voc")))
    return jax.shard_map(
        per_device, mesh=mesh, in_specs=in_specs, out_specs=out_specs, check_vma=False
    )
```

profile of v0, /device:TPU:0, one launch (start us, length us, event | category | flops | bytes accessed | tf_op | source)
XLA Modules:
  0.0 245.8 jit_solution(10150307395011715973)
XLA Ops:
  7.2 0.0 copy-start
  7.2 0.0 all-gather.2.cloned.1.call-start
  7.2 0.7 all-gather.2.cloned.1.call-update
  7.9 0.0 reduce-scatter.3.cloned.1.call-start
  8.0 1.2 dynamic-slice
  9.9 0.9 dynamic-update-slice
  10.7 0.8 dynamic-update-slice.1
  11.6 13.2 %all-reduce.2 = (s32[256]{0:T(256)S(1)}, s32[256]{0:T(256)S(1)}) all-reduce(s32[256]{0:T(256)S(1)} %dynamic-update-slice, s32[256]{0:T(256)S(1)} %dynamic-update-slice.1), channel_id=1, replica_groups=mesh['tok'=8,'voc'=4] {'tok'}, use_global_device_ids=true, to_apply=%add | all-reduce | flops 512 | bytes 4096
  24.8 1.1 reduce_max.24
  25.9 33.4 %all-gather.2.cloned.1.call-done = bf16[256,3584]{1,0:T(8,128)(2,1)} async-done(((bf16[32,3584]{1,0:T(8,128)(2,1)}), bf16[256,3584]{1,0:T(8,128)(2,1)}) %all-gather.2.cloned.1.call-update) | async-done | bytes 1835024 | tf_op jit(solution)/shard_map/all_gather | solution.py:9
  59.3 4.5 %fusion.14 = (f32[256]{0:T(256)S(1)}, f32[256,640]{1,0:T(8,128)S(1)}) fusion(bf16[256,3584]{1,0:T(8,128)(2,1)} %all-gather.2.cloned.1.call-done, bf16[3584,640]{1,0:T(8,128)(2,1)} %param.9), kind=kOutput, calls=%fused_computation.27 | convolution fusion | flops 1174568704 | bytes 7078912 | tf_op jit(solution)/shard_map/dot_general | solution.py:14
  63.8 39.5 %all-reduce.4 = (f32[256]{0:T(256)S(1)}, f32[256]{0:T(256)S(1)}) all-reduce(bf16[256]{0:T(256)(128)(2,1)S(1)} %reduce_max.24, f32[256]{0:T(256)S(1)} %get-tuple-element.28), channel_id=1, replica_groups=mesh['tok'=8,'voc'=4] {'tok','voc'}, use_global_device_ids=true, to_apply=%region_7.0 | all-reduce | flops 512 | bytes 3584 | tf_op jit(solution)/shard_map/pmax | solution.py:24
  103.3 0.0 copy-done
  103.3 0.7 fusion.3
  104.0 39.8 %all-reduce.3 = (f32[256]{0:T(256)S(1)}, f32[256]{0:T(256)S(1)}, f32[256]{0:T(256)S(1)}, f32[256]{0:T(256)S(1)}, f32[256]{0:T(256)S(1)}) all-reduce(f32[256]{0:T(256)S(1)} %get-tuple-element.12, f32[256]{0:T(256)S(1)} %get-tuple-element.9, f32[256]{0:T(256)S(1)} %get-tuple-element.8, ...), channel_id=1, replica_groups=mesh['tok'=8,'voc'=4] {'tok','voc'}, use_global_device_ids=true, to_apply=%region_9.10 | all-reduce | flops 1280 | bytes 10240 | tf_op jit(solution)/shard_map/psum | solution.py:28
  143.7 0.6 convert_reduce_fusion
  144.3 0.0 copy-start.1
  144.4 5.4 %convolution_convert_fusion.1 = bf16[256,3584]{1,0:T(8,128)(2,1)} fusion(bf16[3584,640]{1,0:T(8,128)(2,1)} %param.9, bf16[256,640]{1,0:T(8,128)(2,1)S(1)} %copy-done, f32[256,640]{1,0:T(8,128)S(1)} %get-tuple-element.29, f32[256]{0:T(256)S(1)} %get-tuple-element.27, f32[256]{0:T(256)S(1)} %get-tuple-element.26, f32[256]{0:T(256)S(1)} %get-tuple-element.25, ...), kind=kOutput, calls=%fused_computation.2 | convolution fusion | flops 1176633344 | bytes 7409664 | tf_op jit(solution)/shard_map/dot_general | solution.py:50
  149.8 0.0 reduce-scatter.3.cloned.1.call-update
  149.8 0.0 reduce-scatter.5.cloned.1.call-start
  149.8 66.3 %reduce-scatter.3.cloned.1.call-done = bf16[32,3584]{1,0:T(8,128)(2,1)} async-done(((bf16[256,3584]{1,0:T(8,128)(2,1)}), bf16[32,3584]{1,0:T(8,128)(2,1)}) %reduce-scatter.3.cloned.1.call-update) | async-done | bytes 229392 | tf_op jit(solution)/shard_map/reduce_scatter | solution.py:49
  216.2 0.0 reduce-scatter.5.cloned.1.call-update
  216.2 0.0 copy-done.1
  216.2 3.7 %fusion = bf16[3584,640]{0,1:T(8,128)(2,1)} fusion(bf16[256,3584]{1,0:T(8,128)(2,1)S(1)} %copy-done.1, bf16[256,640]{1,0:T(8,128)(2,1)S(1)} %copy-done, f32[256,640]{1,0:T(8,128)S(1)} %get-tuple-element.29, f32[256]{0:T(256)S(1)} %get-tuple-element.27, f32[256]{0:T(256)S(1)} %get-tuple-element.26, f32[256]{0:T(256)S(1)} %get-tuple-element.25, ...), kind=kOutput, calls=%fused_computation.1 | convolution fusion | flops 1178009600 | bytes 7409664 | tf_op jit(solution)/shard_map/dot_general | solution.py:61
  219.9 7.3 %copy.9 = bf16[3584,640]{1,0:T(8,128)(2,1)} copy(bf16[3584,640]{0,1:T(8,128)(2,1)} %fusion) | data formatting | bytes 9175040
  228.5 0.6 dynamic_slice.3
  229.1 9.0 %reduce-scatter.5.cloned.1.call-done = bf16[8,3584]{1,0:T(8,128)(2,1)} async-done(((bf16[32,3584]{1,0:T(8,128)(2,1)}), bf16[8,3584]{1,0:T(8,128)(2,1)}) %reduce-scatter.5.cloned.1.call-update) | async-done | bytes 57360 | tf_op jit(solution)/shard_map/reduce_scatter | solution.py:57
  (5 shorter events, 0.0 us)
Async XLA Ops:
  7.2 96.1 %copy-start = (bf16[256,640]{1,0:T(8,128)(2,1)S(1)}, bf16[256,640]{1,0:T(8,128)(2,1)}, u32[]{:S(2)}) copy-start(bf16[256,640]{1,0:T(8,128)(2,1)} %param.6) | copy-start | bytes 983044
  7.2 52.1 %all-gather.2.cloned.1.call-start = ((), (), s32[]{:S(2)}) async-start(), calls=%async_computation.2 | async-start | bytes 2064384 | tf_op jit(solution)/shard_map/all_gather | solution.py:9
  7.9 208.2 %reduce-scatter.3.cloned.1.call-start = ((), (), s32[]{:S(2)}) async-start(), calls=%async_computation.3 | async-start | bytes 2064384 | tf_op jit(solution)/shard_map/reduce_scatter | solution.py:49
  144.3 71.8 %copy-start.1 = (bf16[256,3584]{1,0:T(8,128)(2,1)S(1)}, bf16[256,3584]{1,0:T(8,128)(2,1)}, u32[]{:S(2)}) copy-start(bf16[256,3584]{1,0:T(8,128)(2,1)} %all-gather.2.cloned.1.call-done) | copy-start | bytes 5505028
  149.8 88.3 %reduce-scatter.5.cloned.1.call-start = ((), (), s32[]{:S(2)}) async-start(), calls=%async_computation.4 | async-start | bytes 286720 | tf_op jit(solution)/shard_map/reduce_scatter | solution.py:57
Sparse Core Ops, SparseCore 0:
  10.2 49.0 all-gather.1
  149.9 66.1 reduce-scatter.2
  219.2 18.8 reduce-scatter.4
where the time goes:
time: 246 us
  waiting for transfers between devices  109 us (44%)
  blocking collectives  92.4 us (38%)
  between operations  16.9 us (7%)
  matrix products  13.6 us (6%)
  local copies, waits for them, and re-layouts  10.8 us (4%)
    reduce_scatter x1, waiting for transfers between devices, per_device(): lax.psum_scatter(lax.dot_general(dlogits, student_head, (((1,), (1,)), ((...  66.3 us
    psum x1, blocking collectives, per_device(): lax.psum((jnp.sum(shifted, axis=1), jnp.sum(jnp.exp(teacher - teacher_max...  39.8 us
    pmax x1, blocking collectives, per_device(): lax.pmax((jnp.max(student, axis=1), jnp.max(teacher, axis=1)), ('tok', 'v...  39.5 us
    all_gather x1, waiting for transfers between devices, per_device(): lax.all_gather(hidden, 'tok', axis=0, tiled=True)  33.4 us
    unnamed x1, blocking collectives  13.2 us
    unnamed x10, local copies, waits for them, and re-layouts  10.2 us
    reduce_scatter x1, waiting for transfers between devices, per_device(): lax.psum_scatter(partial_sum, 'voc', scatter_dimension=0, tiled=True)  9 us
    dot_general x1, matrix products, per_device(): lax.dot_general(dlogits, student_head, (((1,), (1,)), ((), ())), preferre...  5.42 us
  transfers between devices with their start and end apart: 3, of which 3 were waited for; matrix products, arithmetic and copies ran while one was open for 6% of the time, Pallas kernels for 0%

commit v1 on v0

v1 whole, which is shorter than its diff:
```python
import functools

import jax
import jax.numpy as jnp
from jax import lax
from jax.experimental import pallas as pl
from jax.experimental.pallas import tpu as pltpu
from jax.sharding import PartitionSpec as P

MESH = pl.DeviceIdType.MESH
F32 = jnp.float32
BF16 = jnp.bfloat16
LOW = -3.0e38


def columns_of(parts, rows):
    block = jnp.concatenate(parts + [jnp.zeros((8 - len(parts), rows), F32)], axis=0)
    block = jnp.concatenate([block, jnp.zeros((120, rows), F32)], axis=0)
    return jnp.transpose(block)


def rows_of(parts, rows):
    lane = lax.broadcasted_iota(jnp.int32, (rows, 128), 1)
    block = jnp.zeros((rows, 128), F32)
    for i, part in enumerate(parts):
        block = jnp.where(lane == i, part, block)
    return jnp.transpose(block)


def kernel(
    T, V, WA, WB, NCH,
    hidden, teacher_hbm, code_in, head_hbm,
    small_out, hgrad_out, wgrad_out,
    hid, head, teacher, code, student, tst, sst, cols, dl, dlp, acc,
    cs, cr, s1, r1, s2, r2, zs, zr, hg, wg,
    load_sem, zsem_s, zsem_r, xsem_s, xsem_r, ysem_s, ysem_r, csem_s, csem_r,
    code_s, code_r, ts_s, ts_r, ss_s, ss_r,
    rc_s, rc_r, r1_s, r1_r, r2_s, r2_r, rz_s, rz_r, wsem, osem,
):
    N = T * V
    G = T // 2
    RB, D = hidden.shape
    VD = head_hbm.shape[1]
    R = T * RB
    t, v = lax.axis_index("tok"), lax.axis_index("voc")
    me = t * V + v
    g, x = t // 2, t % 2
    y, c = v // 2, v % 2

    own_load = pltpu.make_async_copy(hidden, hid.at[t], load_sem.at[0])
    own_load.start()
    teacher_load = pltpu.make_async_copy(teacher_hbm, teacher, load_sem.at[1])
    teacher_load.start()
    code_load = pltpu.make_async_copy(code_in, code.at[t], load_sem.at[3])
    code_load.start()
    head_load = pltpu.make_async_copy(head_hbm, head, load_sem.at[2])
    head_load.start()

    barrier = pltpu.get_barrier_semaphore()

    def greet(j, carry):
        peer = lax.rem(me + j, N)
        pl.semaphore_signal(
            barrier, inc=1, device_id={"tok": peer // V, "voc": peer % V}, device_id_type=MESH
        )
        return carry

    lax.fori_loop(1, N, greet, 0)
    own_load.wait()
    code_load.wait()
    pl.semaphore_wait(barrier, N - 1)

    started = []

    def send(src, dst, s_sem, r_sem, to):
        copy = pltpu.make_async_remote_copy(
            src_ref=src, dst_ref=dst, send_sem=s_sem, recv_sem=r_sem,
            device_id=to, device_id_type=MESH,
        )
        copy.start()
        started.append(copy)
        return copy

    def a_cols(q):
        return pl.ds(pl.multiple_of(q * WA, 128), WA)

    def b_cols(q):
        return pl.ds(pl.multiple_of(V * WA + q * WB, 128), WB)

    def pieces(block):
        return (hid.at[block, :, a_cols(v)], hid.at[block, :, b_cols(c)])

    other_x = {"tok": g * 2 + 1 - x, "voc": v}
    other_y = {"tok": t, "voc": (1 - y) * 2 + c}
    other_c = {"tok": t, "voc": y * 2 + 1 - c}

    order = [1] + ([G - 1] if G > 2 else []) + list(range(2, G - 1))
    zcopies, xcopies, ycopies, ccopies = {}, {}, {}, {}
    for p, ref in enumerate(pieces(t)):
        xcopies[0, p] = send(ref, ref, xsem_s.at[0, p], xsem_r.at[0, p], other_x)
    for k in order:
        for p, ref in enumerate(pieces(t)):
            zcopies[k, p] = send(
                ref, ref, zsem_s.at[k, p], zsem_r.at[k, p],
                {"tok": lax.rem(g + k, G) * 2 + x, "voc": v},
            )

    def code_send(j, carry):
        pltpu.make_async_remote_copy(
            src_ref=code.at[t], dst_ref=code.at[t], send_sem=code_s.at[j], recv_sem=code_r.at[j],
            device_id={"tok": lax.rem(t + j, T), "voc": v}, device_id_type=MESH,
        ).start()
        return carry

    lax.fori_loop(1, T, code_send, 0)

    def exchange_start(buf, s_sems, r_sems):
        def body(j, carry):
            peer = lax.rem(me + j, N)
            pltpu.make_async_remote_copy(
                src_ref=buf.at[me], dst_ref=buf.at[me], send_sem=s_sems.at[j],
                recv_sem=r_sems.at[j],
                device_id={"tok": peer // V, "voc": peer % V}, device_id_type=MESH,
            ).start()
            return carry

        lax.fori_loop(1, N, body, 0)

    def exchange_wait(buf, s_sems, r_sems):
        def body(j, carry):
            source = lax.rem(me + N - j, N)
            pltpu.make_async_remote_copy(
                src_ref=buf.at[me], dst_ref=buf.at[source], send_sem=s_sems.at[j],
                recv_sem=r_sems.at[j],
                device_id={"tok": source // V, "voc": source % V}, device_id_type=MESH,
            ).wait()
            return carry

        lax.fori_loop(1, N, body, 0)

    teacher_load.wait()
    tl = teacher[...].astype(F32)
    t_max = jnp.max(tl, axis=1, keepdims=True)
    t_sum = jnp.sum(jnp.exp(tl - t_max), axis=1, keepdims=True)
    tst[me] = rows_of([t_max, t_sum], R)[0:2]
    exchange_start(tst, ts_s, ts_r)

    def landed(copies, key):
        copies[key].wait_recv()

    def forward(block, index, base, to_x):
        refs = pieces(block)
        if to_x:
            for p, ref in enumerate(refs):
                xcopies[index, p] = send(ref, ref, xsem_s.at[index, p], xsem_r.at[index, p], other_x)
        ref = refs[0]
        ycopies[base] = send(ref, ref, ysem_s.at[base], ysem_r.at[base], other_y)
        for p, ref in enumerate(refs):
            ccopies[base, p] = send(ref, ref, csem_s.at[base, p], csem_r.at[base, p], other_c)

    def x_landed(k):
        for p in range(2):
            landed(xcopies, (k, p))
        forward(lax.rem(g + G - k, G) * 2 + 1 - x, None, G + k, False)

    x_landed(0)
    for k in order:
        for p in range(2):
            landed(zcopies, (k, p))
        forward(lax.rem(g + G - k, G) * 2 + x, k, k, True)
    for k in order:
        x_landed(k)

    flat = hid.reshape(R, D)

    def part(where):
        return jnp.dot(flat[:, where], head[where, :], preferred_element_type=F32)

    head_load.wait()
    student[...] = part(a_cols(v)) + part(b_cols(c))
    for base in [G] + order + [G + k for k in order]:
        landed(ycopies, base)
        shift = base % G
        block = lax.rem(g + G - shift, G) * 2 + (x if base < G else 1 - x)
        ref = hid.at[block, :, a_cols((1 - y) * 2 + c)]
        ccopies[base, 2] = send(ref, ref, csem_s.at[base, 2], csem_r.at[base, 2], other_c)
        for p in range(2):
            landed(ccopies, (base, p))
    student[...] += part(a_cols((1 - y) * 2 + c))
    student[...] += part(a_cols(y * 2 + 1 - c)) + part(b_cols(1 - c))

    exchange_wait(tst, ts_s, ts_r)
    tm = tst[:, 0, :]
    tm_all = jnp.max(tm, axis=0, keepdims=True)
    ts_all = jnp.sum(jnp.exp(tm - tm_all) * tst[:, 1, :], axis=0, keepdims=True)
    tcol = columns_of([tm_all, jnp.log(ts_all)], R)
    lt = (teacher[...].astype(F32) - tcol[:, 0:1]) - tcol[:, 1:2]

    def code_wait(j, carry):
        source = lax.rem(t + T - j, T)
        pltpu.make_async_remote_copy(
            src_ref=code.at[t], dst_ref=code.at[source], send_sem=code_s.at[j],
            recv_sem=code_r.at[j], device_id={"tok": source, "voc": v}, device_id_type=MESH,
        ).wait()
        return carry

    lax.fori_loop(1, T, code_wait, 0)
    diagonal = lax.broadcasted_iota(jnp.int32, (RB, 128), 1) == lax.broadcasted_iota(
        jnp.int32, (RB, 128), 0
    )

    def column(row):
        return jnp.concatenate(
            [
                jnp.sum(jnp.where(diagonal, code[i, row : row + 1, :], 0.0), axis=1, keepdims=True)
                for i in range(T)
            ],
            axis=0,
        )

    ids = column(0)
    weight = column(1)
    mine = (me * VD + lax.broadcasted_iota(jnp.int32, (1, VD), 1)).astype(F32)
    chosen = ids == mine

    for base in [G] + order + [G + k for k in order]:
        landed(ccopies, (base, 2))
    s = student[...] + part(a_cols((1 - y) * 2 + 1 - c))
    student[...] = s
    s_max = jnp.max(s, axis=1, keepdims=True)
    rel = s - s_max
    e = jnp.exp(rel)
    diff = rel - lt
    s_sum = jnp.sum(e, axis=1, keepdims=True)
    cross = jnp.sum(e * diff, axis=1, keepdims=True)
    pick = jnp.max(jnp.where(chosen, diff, LOW), axis=1, keepdims=True)
    sst[me] = rows_of([s_max, s_sum, cross, pick], R)[0:4]
    exchange_start(sst, ss_s, ss_r)
    exchange_wait(sst, ss_s, ss_r)
    sm = sst[:, 0, :]
    ss = sst[:, 1, :]
    sm_all = jnp.max(sm, axis=0, keepdims=True)
    move = sm - sm_all
    scale = jnp.exp(move)
    total = jnp.sum(scale * ss, axis=0, keepdims=True)
    cross_all = jnp.sum(scale * (sst[:, 2, :] + ss * move), axis=0, keepdims=True)
    pick_all = jnp.max(sst[:, 3, :] + move, axis=0, keepdims=True)
    log_total = jnp.log(total)
    kl = cross_all / total - log_total
    ratio = pick_all - log_total
    scol = columns_of([sm_all, log_total, kl, ratio], R)
    kl_c = scol[:, 2:3]
    count = jnp.sum(weight, axis=0, keepdims=True)
    loss = jnp.sum(weight * kl_c, axis=0, keepdims=True) / count
    cols[...] = scol
    small_out[0] = cols[pl.ds(pl.multiple_of(me * (R // N), 8), R // N), :]
    small_out[1] = jnp.broadcast_to(loss, (R // N, 128))
    ls = (student[...] - scol[:, 0:1]) - scol[:, 1:2]
    d = weight * jnp.exp(ls) * ((ls - lt) - kl_c)
    dl[...] = d.astype(BF16)
    RO = R // N
    dlp[...] = (
        d.reshape(G, 2, 2, 2, RO, VD).transpose(3, 2, 1, 0, 4, 5).reshape(2, R // 2, VD).astype(BF16)
    )

    CW = D // NCH
    turns = [i for pair in zip(range(NCH // 2), range(NCH // 2, NCH)) for i in pair]
    H = R // 8
    other = ((1,), (1,))

    def grad_part(which, ch):
        return lax.dot_general(
            dlp[which], head[pl.ds(ch * CW, CW), :], (other, ((), ())), preferred_element_type=F32
        )

    hops = {}
    for ch in turns:
        cs[ch] = grad_part(1 - c, ch).astype(BF16)
        hops["c", ch] = send(cs.at[ch], cr.at[ch], rc_s.at[ch], rc_r.at[ch], other_c)
    for ch in turns:
        acc[ch] = grad_part(c, ch).reshape(2, 2, H, CW)
    wchunks = 7 if D % 7 == 0 else 1
    WC = D // wchunks
    wdone = []

    def weight_grad(i):
        rows = pl.ds(i * WC, WC)
        wg[rows, :] = lax.dot_general(
            flat[:, rows], dl[...], (((0,), (0,)), ((), ())), preferred_element_type=F32
        ).astype(BF16)
        copy = pltpu.make_async_copy(wg.at[rows, :], wgrad_out.at[rows, :], wsem.at[i])
        copy.start()
        wdone.append(copy)

    for ch in turns:
        hops["c", ch].wait_recv()
        acc[ch] += cr[ch].astype(F32).reshape(2, 2, H, CW)
        if ch < NCH // 2:
            s1[ch] = acc[ch, 1 - y].astype(BF16)
            to = other_y
        else:
            s1[ch] = acc[ch, :, 1 - x].astype(BF16)
            to = other_x
        hops["1", ch] = send(s1.at[ch], r1.at[ch], r1_s.at[ch], r1_r.at[ch], to)
    for i in range(0, 3 * wchunks // 7):
        weight_grad(i)
    for ch in turns:
        hops["1", ch].wait_recv()
        got = r1[ch].astype(F32)
        if ch < NCH // 2:
            acc[ch, y] += got
            s2[ch] = acc[ch, y, 1 - x].astype(BF16)
            to = other_x
        else:
            acc[ch, :, x] += got
            s2[ch] = acc[ch, 1 - y, x].astype(BF16)
            to = other_y
        hops["2", ch] = send(s2.at[ch], r2.at[ch], r2_s.at[ch], r2_r.at[ch], to)
    for i in range(3 * wchunks // 7, 5 * wchunks // 7):
        weight_grad(i)
    half = CW // 2
    for ch in turns:
        hops["2", ch].wait_recv()
        both = acc[ch, y, x] + r2[ch].astype(F32)
        for i in range(G):
            rows = both[i * RO : (i + 1) * RO]
            acc[ch, 0, 0, i * RO : (i + 1) * RO, :] = rows
            zs[ch, i] = jnp.concatenate([rows[:, :half], rows[:, half:]], axis=0).astype(BF16)
        for k in order:
            to = lax.rem(g + k, G)
            hops["z", ch, k] = send(
                zs.at[ch, to], zr.at[ch, k], rz_s.at[ch, k], rz_r.at[ch, k],
                {"tok": to * 2 + x, "voc": v},
            )
    for i in range(5 * wchunks // 7, wchunks):
        weight_grad(i)
    for ch in turns:
        mine_rows = acc[ch, 0, 0, pl.ds(pl.multiple_of(g * RO, 8), RO), :]
        for k in order:
            hops["z", ch, k].wait_recv()
            got = zr[ch, k].astype(F32)
            mine_rows = mine_rows + jnp.concatenate([got[:RO], got[RO:]], axis=1)
        hgrad_out[:, ch * CW : (ch + 1) * CW] = mine_rows.astype(BF16)
    for copy in started:
        copy.wait_send()
    for copy in wdone:
        copy.wait()


def per_device(T, V, hidden, teacher_logits, sampled_ids, loss_mask, student_head):
    RB, D = hidden.shape
    VD = student_head.shape[1]
    N, G, R = T * V, T // 2, T * RB
    RO = R // N
    units = D // 128
    a = (units * 5) // 28
    b = (units - V * a) // 2
    WA, WB = a * 128, b * 128
    NCH = 4
    CW = D // NCH
    code = jnp.pad(
        jnp.stack([sampled_ids, loss_mask]).astype(F32), ((0, 6), (0, 128 - RB))
    )
    DMA = pltpu.SemaphoreType.DMA
    H = R // 8
    any_space = pl.BlockSpec(memory_space=pl.ANY)
    vmem = pl.BlockSpec(memory_space=pltpu.VMEM)
    small, hidden_grad, head_grad = pl.pallas_call(
        functools.partial(kernel, T, V, WA, WB, NCH),
        out_shape=(
            jax.ShapeDtypeStruct((2, RO, 128), F32),
            jax.ShapeDtypeStruct((RO, D), BF16),
            jax.ShapeDtypeStruct((D, VD), BF16),
        ),
        in_specs=[any_space] * 4,
        out_specs=(vmem, vmem, any_space),
        scratch_shapes=[
            pltpu.VMEM((T, RB, D), BF16),
            pltpu.VMEM((D, VD), BF16),
            pltpu.VMEM((R, VD), BF16),
            pltpu.VMEM((T, 8, 128), F32),
            pltpu.VMEM((R, VD), F32),
            pltpu.VMEM((N, 2, R), F32),
            pltpu.VMEM((N, 4, R), F32),
            pltpu.VMEM((R, 128), F32),
            pltpu.VMEM((R, VD), BF16),
            pltpu.VMEM((2, R // 2, VD), BF16),
            pltpu.VMEM((NCH, 2, 2, H, CW), F32),
            pltpu.VMEM((NCH, R // 2, CW), BF16),
            pltpu.VMEM((NCH, R // 2, CW), BF16),
            pltpu.VMEM((NCH, 2, H, CW), BF16),
            pltpu.VMEM((NCH, 2, H, CW), BF16),
            pltpu.VMEM((NCH, H, CW), BF16),
            pltpu.VMEM((NCH, H, CW), BF16),
            pltpu.VMEM((NCH, G, 2 * RO, CW // 2), BF16),
            pltpu.VMEM((NCH, G, 2 * RO, CW // 2), BF16),
            pltpu.VMEM((8, 128), F32),
            pltpu.VMEM((D, VD), BF16),
            DMA((4,)),
            DMA((G, 2)), DMA((G, 2)),
            DMA((G, 2)), DMA((G, 2)),
            DMA((T,)), DMA((T,)),
            DMA((T, 3)), DMA((T, 3)),
            DMA((T,)), DMA((T,)),
            DMA((N,)), DMA((N,)),
            DMA((N,)), DMA((N,)),
            DMA((NCH,)), DMA((NCH,)),
            DMA((NCH,)), DMA((NCH,)),
            DMA((NCH,)), DMA((NCH,)),
            DMA((NCH, G)), DMA((NCH, G)),
            DMA((7,)),
            DMA((1,)),
        ],
        compiler_params=pltpu.CompilerParams(
            collective_id=0, has_side_effects=True, vmem_limit_bytes=60 * 1024 * 1024
        ),
    )(hidden, teacher_logits, code, student_head)
    return small[1, 0, 0], small[0, :, 3], hidden_grad, head_grad


def solution(mesh):
    in_specs = (
        P("tok", None),
        P(None, ("tok", "voc")),
        P("tok"),
        P("tok"),
        P(None, ("tok", "voc")),
    )
    out_specs = (P(), P(("tok", "voc")), P(("tok", "voc"), None), P(None, ("tok", "voc")))
    return jax.shard_map(
        functools.partial(per_device, mesh.shape["tok"], mesh.shape["voc"]),
        mesh=mesh, in_specs=in_specs, out_specs=out_specs, check_vma=False,
    )
```

time: 246 us -> 64.5 us (0.26)
  waiting for transfers between devices: 109 us -> 0 us
  blocking collectives: 92.4 us -> 0 us
  Pallas kernels: 0 us -> 53.4 us
  between operations: 16.9 us -> 0.64 us
  matrix products: 13.6 us -> 0 us
    reduce_scatter x2 -> x0, waiting for transfers between devices: 75.3 us -> none  [the longest x1 66.3 us: per_device(): lax.psum_scatter(lax.dot_general(dlogits, student_head, (((1,), (1,)), ((...]
    pallas_call x0 -> x1, Pallas kernels: none -> 53.4 us  [per_device(): pl.pallas_call(functools.partial(kernel, T, V, WA, WB, NCH), out_shape=(j...]
    psum x1 -> x0, blocking collectives: 39.8 us -> none  [per_device(): lax.psum((jnp.sum(shifted, axis=1), jnp.sum(jnp.exp(teacher - teacher_max...]
    pmax x1 -> x0, blocking collectives: 39.5 us -> none  [per_device(): lax.pmax((jnp.max(student, axis=1), jnp.max(teacher, axis=1)), ('tok', 'v...]
    all_gather x1 -> x0, waiting for transfers between devices: 33.4 us -> none  [per_device(): lax.all_gather(hidden, 'tok', axis=0, tiled=True)]
    dot_general x3 -> x0, matrix products: 13.6 us -> none  [the longest x1 5.42 us: per_device(): lax.dot_general(dlogits, student_head, (((1,), (1,)), ((), ())), preferre...]
    unnamed x1 -> x0, blocking collectives: 13.2 us -> none
    unnamed x10 -> x2, local copies, waits for them, and re-layouts: 10.2 us -> 6.28 us
  transfers between devices with their start and end apart: 3 -> 0, of which waited for: 3 -> 0; matrix products, arithmetic and copies ran while one was open for 6% -> 0% of each run, Pallas kernels for 0% -> 0%
where the time goes in v1:
time: 64.5 us; the launch traced here: 64.2 us
  Pallas kernels  53.4 us (83%)
  local copies, waits for them, and re-layouts  9.43 us (15%)
  other arithmetic  0.68 us (1%)
    pallas_call x1, Pallas kernels, per_device(): pl.pallas_call(functools.partial(kernel, T, V, WA, WB, NCH), out_shape=(j...  53.4 us
    unnamed x2, local copies, waits for them, and re-layouts  6.28 us
    slice x2, local copies, waits for them, and re-layouts, per_device(): return (small[1, 0, 0], small[0, :, 3], hidden_grad, head_grad)  2.56 us

profile of v1, /device:TPU:0, one launch (start us, length us, event | category | flops | bytes accessed | tf_op | source)
XLA Modules:
  0.0 64.2 jit_solution(17351312901767882952)
XLA Ops:
  0.6 0.7 %add_convert_fusion = f32[2,32]{1,0:T(2,128)S(1)} fusion(s32[1,32]{1,0:T(1,128)} %bitcast.3, s32[1,32]{1,0:T(1,128)} %bitcast.4), kind=kLoop, calls=%fused_computation.1 | loop fusion | flops 128 | bytes 512 | tf_op jit(solution)/shard_map/convert_element_type | solution.py:362
  1.3 0.6 pad.4.code_in
  1.9 53.4 %shard_map.84 = (f32[2,8,128]{2,1,0:T(8,128)}, bf16[8,3584]{1,0:T(8,128)(2,1)}, bf16[3584,640]{1,0:T(8,128)(2,1)}) custom-call(bf16[32,3584]{1,0:T(8,128)(2,1)} %hidden.1, bf16[256,640]{1,0:T(8,128)(2,1)} %teacher_hbm.1, f32[8,128]{1,0:T(8,128)} %pad.4.code_in, bf16[3584,640]{1,0:T(8,128)(2,1)} %head_hbm.1), custom_call_target="tpu_custom_call" | custom-call | tf_op jit(solution)/shard_map/pallas_call | solution.py:368
  55.4 1.2 %slice.6 = f32[1,1,1]{2,1,0:T(1,128)} slice(f32[2,8,128]{2,1,0:T(8,128)} %get-tuple-element.7), slice={[1:2], [0:1], [0:1]} | slice | bytes 8 | tf_op jit(solution)/shard_map/slice | solution.py:418
  56.5 1.4 %slice_reduce_fusion = f32[8]{0:T(128)} fusion(f32[2,8,128]{2,1,0:T(8,128)} %get-tuple-element.7), kind=kLoop, calls=%fused_computation | loop fusion | bytes 64 | tf_op jit(solution)/shard_map/slice | solution.py:418
  57.9 1.4 %copy.11 = bf16[8,3584]{1,0:T(8,128)(2,1)} copy(bf16[8,3584]{1,0:T(8,128)(2,1)} %get-tuple-element.16) | data formatting | bytes 114688
  59.4 4.8 %copy.12 = bf16[3584,640]{1,0:T(8,128)(2,1)} copy(bf16[3584,640]{1,0:T(8,128)(2,1)} %get-tuple-element.17) | data formatting | bytes 9175040

commit v2 on v1

--- a/solution.py
+++ b/solution.py
@@ -29,13 +29,13 @@
 
 def kernel(
     T, V, WA, WB, NCH,
-    hidden, teacher_hbm, code_in, head_hbm,
-    small_out, hgrad_out, wgrad_out,
+    hidden, teacher_hbm, ids_in, mask_in, head_hbm,
+    loss_out, ratio_out, hgrad_out, wg,
     hid, head, teacher, code, student, tst, sst, cols, dl, dlp, acc,
-    cs, cr, s1, r1, s2, r2, zs, zr, hg, wg,
+    cs, cr, s1, r1, s2, r2, zs, zr,
     load_sem, zsem_s, zsem_r, xsem_s, xsem_r, ysem_s, ysem_r, csem_s, csem_r,
-    code_s, code_r, ts_s, ts_r, ss_s, ss_r,
-    rc_s, rc_r, r1_s, r1_r, r2_s, r2_r, rz_s, rz_r, wsem, osem,
+    kz_s, kz_r, kx_s, kx_r, ts_s, ts_r, ss_s, ss_r,
+    rc_s, rc_r, r1_s, r1_r, r2_s, r2_r, rz_s, rz_r,
 ):
     N = T * V
     G = T // 2
@@ -51,24 +51,28 @@
     own_load.start()
     teacher_load = pltpu.make_async_copy(teacher_hbm, teacher, load_sem.at[1])
     teacher_load.start()
-    code_load = pltpu.make_async_copy(code_in, code.at[t], load_sem.at[3])
-    code_load.start()
+    ids_load = pltpu.make_async_copy(ids_in, code.at[t, 0], load_sem.at[3])
+    ids_load.start()
+    mask_load = pltpu.make_async_copy(mask_in, code.at[t, 1], load_sem.at[4])
+    mask_load.start()
     head_load = pltpu.make_async_copy(head_hbm, head, load_sem.at[2])
     head_load.start()
 
     barrier = pltpu.get_barrier_semaphore()
 
-    def greet(j, carry):
-        peer = lax.rem(me + j, N)
-        pl.semaphore_signal(
-            barrier, inc=1, device_id={"tok": peer // V, "voc": peer % V}, device_id_type=MESH
-        )
-        return carry
-
-    lax.fori_loop(1, N, greet, 0)
+    other_x = {"tok": g * 2 + 1 - x, "voc": v}
+    other_y = {"tok": t, "voc": (1 - y) * 2 + c}
+    other_c = {"tok": t, "voc": y * 2 + 1 - c}
+
+    def other_z(k):
+        return {"tok": lax.rem(g + k, G) * 2 + x, "voc": v}
+
+    for peer in [other_z(k) for k in range(1, G)] + [other_y, other_x, other_c]:
+        pl.semaphore_signal(barrier, inc=1, device_id=peer, device_id_type=MESH)
     own_load.wait()
-    code_load.wait()
-    pl.semaphore_wait(barrier, N - 1)
+    ids_load.wait()
+    mask_load.wait()
+    pl.semaphore_wait(barrier, G + 2)
 
     started = []
 
@@ -90,29 +94,26 @@
     def pieces(block):
         return (hid.at[block, :, a_cols(v)], hid.at[block, :, b_cols(c)])
 
-    other_x = {"tok": g * 2 + 1 - x, "voc": v}
-    other_y = {"tok": t, "voc": (1 - y) * 2 + c}
-    other_c = {"tok": t, "voc": y * 2 + 1 - c}
-
     order = [1] + ([G - 1] if G > 2 else []) + list(range(2, G - 1))
     zcopies, xcopies, ycopies, ccopies = {}, {}, {}, {}
+    kzcopies, kxcopies = {}, {}
+
+    def code_to_x(block, k):
+        ref = code.at[block]
+        kxcopies[k] = send(ref, ref, kx_s.at[k], kx_r.at[k], other_x)
+
     for p, ref in enumerate(pieces(t)):
         xcopies[0, p] = send(ref, ref, xsem_s.at[0, p], xsem_r.at[0, p], other_x)
     for k in order:
         for p, ref in enumerate(pieces(t)):
             zcopies[k, p] = send(
                 ref, ref, zsem_s.at[k, p], zsem_r.at[k, p],
-                {"tok": lax.rem(g + k, G) * 2 + x, "voc": v},
+                other_z(k),
             )
 
-    def code_send(j, carry):
-        pltpu.make_async_remote_copy(
-            src_ref=code.at[t], dst_ref=code.at[t], send_sem=code_s.at[j], recv_sem=code_r.at[j],
-            device_id={"tok": lax.rem(t + j, T), "voc": v}, device_id_type=MESH,
-        ).start()
-        return carry
-
-    lax.fori_loop(1, T, code_send, 0)
+    code_to_x(t, 0)
+    for k in order:
+        kzcopies[k] = send(code.at[t], code.at[t], kz_s.at[k], kz_r.at[k], other_z(k))
 
     def exchange_start(buf, s_sems, r_sems):
         def body(j, carry):
@@ -143,7 +144,7 @@
     t_max = jnp.max(tl, axis=1, keepdims=True)
     t_sum = jnp.sum(jnp.exp(tl - t_max), axis=1, keepdims=True)
     tst[me] = rows_of([t_max, t_sum], R)[0:2]
-    exchange_start(tst, ts_s, ts_r)
+    t_rel = tl - t_max
 
     def landed(copies, key):
         copies[key].wait_recv()
@@ -168,6 +169,9 @@
         for p in range(2):
             landed(zcopies, (k, p))
         forward(lax.rem(g + G - k, G) * 2 + x, k, k, True)
+    for k in order:
+        landed(kzcopies, k)
+        code_to_x(lax.rem(g + G - k, G) * 2 + x, k)
     for k in order:
         x_landed(k)
 
@@ -189,30 +193,16 @@
     student[...] += part(a_cols((1 - y) * 2 + c))
     student[...] += part(a_cols(y * 2 + 1 - c)) + part(b_cols(1 - c))
 
-    exchange_wait(tst, ts_s, ts_r)
-    tm = tst[:, 0, :]
-    tm_all = jnp.max(tm, axis=0, keepdims=True)
-    ts_all = jnp.sum(jnp.exp(tm - tm_all) * tst[:, 1, :], axis=0, keepdims=True)
-    tcol = columns_of([tm_all, jnp.log(ts_all)], R)
-    lt = (teacher[...].astype(F32) - tcol[:, 0:1]) - tcol[:, 1:2]
-
-    def code_wait(j, carry):
-        source = lax.rem(t + T - j, T)
-        pltpu.make_async_remote_copy(
-            src_ref=code.at[t], dst_ref=code.at[source], send_sem=code_s.at[j],
-            recv_sem=code_r.at[j], device_id={"tok": source, "voc": v}, device_id_type=MESH,
-        ).wait()
-        return carry
-
-    lax.fori_loop(1, T, code_wait, 0)
-    diagonal = lax.broadcasted_iota(jnp.int32, (RB, 128), 1) == lax.broadcasted_iota(
-        jnp.int32, (RB, 128), 0
+    for k in [0] + order:
+        landed(kxcopies, k)
+    diagonal = lax.broadcasted_iota(jnp.int32, (RB, RB), 1) == lax.broadcasted_iota(
+        jnp.int32, (RB, RB), 0
     )
 
     def column(row):
         return jnp.concatenate(
             [
-                jnp.sum(jnp.where(diagonal, code[i, row : row + 1, :], 0.0), axis=1, keepdims=True)
+                jnp.sum(jnp.where(diagonal, code[i, row].astype(F32), 0.0), axis=1, keepdims=True)
                 for i in range(T)
             ],
             axis=0,
@@ -225,17 +215,23 @@
 
     for base in [G] + order + [G + k for k in order]:
         landed(ccopies, (base, 2))
+    exchange_start(tst, ts_s, ts_r)
     s = student[...] + part(a_cols((1 - y) * 2 + 1 - c))
     student[...] = s
     s_max = jnp.max(s, axis=1, keepdims=True)
     rel = s - s_max
     e = jnp.exp(rel)
-    diff = rel - lt
+    diff = rel - t_rel
     s_sum = jnp.sum(e, axis=1, keepdims=True)
     cross = jnp.sum(e * diff, axis=1, keepdims=True)
     pick = jnp.max(jnp.where(chosen, diff, LOW), axis=1, keepdims=True)
     sst[me] = rows_of([s_max, s_sum, cross, pick], R)[0:4]
     exchange_start(sst, ss_s, ss_r)
+    exchange_wait(tst, ts_s, ts_r)
+    tm = tst[:, 0, :]
+    tm_all = jnp.max(tm, axis=0, keepdims=True)
+    tmove = tm - tm_all
+    log_ts = jnp.log(jnp.sum(jnp.exp(tmove) * tst[:, 1, :], axis=0, keepdims=True))
     exchange_wait(sst, ss_s, ss_r)
     sm = sst[:, 0, :]
     ss = sst[:, 1, :]
@@ -243,22 +239,27 @@
     move = sm - sm_all
     scale = jnp.exp(move)
     total = jnp.sum(scale * ss, axis=0, keepdims=True)
-    cross_all = jnp.sum(scale * (sst[:, 2, :] + ss * move), axis=0, keepdims=True)
-    pick_all = jnp.max(sst[:, 3, :] + move, axis=0, keepdims=True)
+    cross_all = jnp.sum(scale * (sst[:, 2, :] + ss * (move - tmove)), axis=0, keepdims=True)
+    pick_all = jnp.max(sst[:, 3, :] + (move - tmove), axis=0, keepdims=True)
     log_total = jnp.log(total)
-    kl = cross_all / total - log_total
-    ratio = pick_all - log_total
-    scol = columns_of([sm_all, log_total, kl, ratio], R)
+    kl = cross_all / total - log_total + log_ts
+    ratio = pick_all - log_total + log_ts
+    scol = columns_of([sm_all, log_total, kl, ratio, tm_all, log_ts], R)
+    lt = (teacher[...].astype(F32) - scol[:, 4:5]) - scol[:, 5:6]
     kl_c = scol[:, 2:3]
     count = jnp.sum(weight, axis=0, keepdims=True)
     loss = jnp.sum(weight * kl_c, axis=0, keepdims=True) / count
     cols[...] = scol
-    small_out[0] = cols[pl.ds(pl.multiple_of(me * (R // N), 8), R // N), :]
-    small_out[1] = jnp.broadcast_to(loss, (R // N, 128))
+    RO = R // N
+    mine_col = cols[pl.ds(pl.multiple_of(me * RO, 8), RO), 3:4]
+    eye = lax.broadcasted_iota(jnp.int32, (RO, RO), 1) == lax.broadcasted_iota(
+        jnp.int32, (RO, RO), 0
+    )
+    ratio_out[...] = jnp.sum(jnp.where(eye, mine_col, 0.0), axis=0, keepdims=True)
+    loss_out[...] = loss
     ls = (student[...] - scol[:, 0:1]) - scol[:, 1:2]
     d = weight * jnp.exp(ls) * ((ls - lt) - kl_c)
     dl[...] = d.astype(BF16)
-    RO = R // N
     dlp[...] = (
         d.reshape(G, 2, 2, 2, RO, VD).transpose(3, 2, 1, 0, 4, 5).reshape(2, R // 2, VD).astype(BF16)
     )
@@ -281,16 +282,12 @@
         acc[ch] = grad_part(c, ch).reshape(2, 2, H, CW)
     wchunks = 7 if D % 7 == 0 else 1
     WC = D // wchunks
-    wdone = []
 
     def weight_grad(i):
         rows = pl.ds(i * WC, WC)
         wg[rows, :] = lax.dot_general(
             flat[:, rows], dl[...], (((0,), (0,)), ((), ())), preferred_element_type=F32
         ).astype(BF16)
-        copy = pltpu.make_async_copy(wg.at[rows, :], wgrad_out.at[rows, :], wsem.at[i])
-        copy.start()
-        wdone.append(copy)
 
     for ch in turns:
         hops["c", ch].wait_recv()
@@ -302,9 +299,11 @@
             s1[ch] = acc[ch, :, 1 - x].astype(BF16)
             to = other_x
         hops["1", ch] = send(s1.at[ch], r1.at[ch], r1_s.at[ch], r1_r.at[ch], to)
-    for i in range(0, 3 * wchunks // 7):
+    for i in range(0, 4 * wchunks // 7):
         weight_grad(i)
-    for ch in turns:
+    half = CW // 2
+
+    def second(ch):
         hops["1", ch].wait_recv()
         got = r1[ch].astype(F32)
         if ch < NCH // 2:
@@ -316,23 +315,27 @@
             s2[ch] = acc[ch, 1 - y, x].astype(BF16)
             to = other_y
         hops["2", ch] = send(s2.at[ch], r2.at[ch], r2_s.at[ch], r2_r.at[ch], to)
-    for i in range(3 * wchunks // 7, 5 * wchunks // 7):
-        weight_grad(i)
-    half = CW // 2
-    for ch in turns:
+
+    def third(ch):
         hops["2", ch].wait_recv()
         both = acc[ch, y, x] + r2[ch].astype(F32)
+        acc[ch, 0, 0] = both
         for i in range(G):
             rows = both[i * RO : (i + 1) * RO]
-            acc[ch, 0, 0, i * RO : (i + 1) * RO, :] = rows
             zs[ch, i] = jnp.concatenate([rows[:, :half], rows[:, half:]], axis=0).astype(BF16)
         for k in order:
-            to = lax.rem(g + k, G)
             hops["z", ch, k] = send(
-                zs.at[ch, to], zr.at[ch, k], rz_s.at[ch, k], rz_r.at[ch, k],
-                {"tok": to * 2 + x, "voc": v},
+                zs.at[ch, lax.rem(g + k, G)], zr.at[ch, k], rz_s.at[ch, k], rz_r.at[ch, k],
+                other_z(k),
             )
-    for i in range(5 * wchunks // 7, wchunks):
+
+    lag = 4 if NCH > 4 else 2
+    for i in range(NCH + lag):
+        if i < NCH:
+            second(turns[i])
+        if i >= lag:
+            third(turns[i - lag])
+    for i in range(4 * wchunks // 7, wchunks):
         weight_grad(i)
     for ch in turns:
         mine_rows = acc[ch, 0, 0, pl.ds(pl.multiple_of(g * RO, 8), RO), :]
@@ -343,7 +346,16 @@
         hgrad_out[:, ch * CW : (ch + 1) * CW] = mine_rows.astype(BF16)
     for copy in started:
         copy.wait_send()
-    for copy in wdone:
+
+
+def store_all(a, b, c, d, oa, ob, oc, od, sem):
+    copies = [
+        pltpu.make_async_copy(src, dst, sem.at[i])
+        for i, (src, dst) in enumerate(((d, od), (c, oc), (b, ob), (a, oa)))
+    ]
+    for copy in copies:
+        copy.start()
+    for copy in copies:
         copy.wait()
 
 
@@ -356,29 +368,25 @@
     a = (units * 5) // 28
     b = (units - V * a) // 2
     WA, WB = a * 128, b * 128
-    NCH = 4
+    NCH = D // 256 if (D // 256) % 2 == 0 else 2
     CW = D // NCH
-    code = jnp.pad(
-        jnp.stack([sampled_ids, loss_mask]).astype(F32), ((0, 6), (0, 128 - RB))
-    )
     DMA = pltpu.SemaphoreType.DMA
     H = R // 8
     any_space = pl.BlockSpec(memory_space=pl.ANY)
     vmem = pl.BlockSpec(memory_space=pltpu.VMEM)
-    small, hidden_grad, head_grad = pl.pallas_call(
+    shapes = (
+        ((1, 1), F32), ((1, RO), F32), ((RO, D), BF16), ((D, VD), BF16),
+    )
+    kept = pl.pallas_call(
         functools.partial(kernel, T, V, WA, WB, NCH),
-        out_shape=(
-            jax.ShapeDtypeStruct((2, RO, 128), F32),
-            jax.ShapeDtypeStruct((RO, D), BF16),
-            jax.ShapeDtypeStruct((D, VD), BF16),
-        ),
-        in_specs=[any_space] * 4,
-        out_specs=(vmem, vmem, any_space),
+        out_shape=tuple(pltpu.VMEM(shape, kind) for shape, kind in shapes),
+        in_specs=[any_space] * 5,
+        out_specs=(vmem,) * 4,
         scratch_shapes=[
             pltpu.VMEM((T, RB, D), BF16),
             pltpu.VMEM((D, VD), BF16),
             pltpu.VMEM((R, VD), BF16),
-            pltpu.VMEM((T, 8, 128), F32),
+            pltpu.VMEM((T, 2, 1, RB), jnp.int32),
             pltpu.VMEM((R, VD), F32),
             pltpu.VMEM((N, 2, R), F32),
             pltpu.VMEM((N, 4, R), F32),
@@ -394,28 +402,35 @@
             pltpu.VMEM((NCH, H, CW), BF16),
             pltpu.VMEM((NCH, G, 2 * RO, CW // 2), BF16),
             pltpu.VMEM((NCH, G, 2 * RO, CW // 2), BF16),
-            pltpu.VMEM((8, 128), F32),
-            pltpu.VMEM((D, VD), BF16),
-            DMA((4,)),
+            DMA((5,)),
             DMA((G, 2)), DMA((G, 2)),
             DMA((G, 2)), DMA((G, 2)),
             DMA((T,)), DMA((T,)),
             DMA((T, 3)), DMA((T, 3)),
-            DMA((T,)), DMA((T,)),
+            DMA((G,)), DMA((G,)),
+            DMA((G,)), DMA((G,)),
             DMA((N,)), DMA((N,)),
             DMA((N,)), DMA((N,)),
             DMA((NCH,)), DMA((NCH,)),
             DMA((NCH,)), DMA((NCH,)),
             DMA((NCH,)), DMA((NCH,)),
             DMA((NCH, G)), DMA((NCH, G)),
-            DMA((7,)),
-            DMA((1,)),
         ],
         compiler_params=pltpu.CompilerParams(
-            collective_id=0, has_side_effects=True, vmem_limit_bytes=60 * 1024 * 1024
+            collective_id=0, has_side_effects=True, vmem_limit_bytes=54 * 1024 * 1024
         ),
-    )(hidden, teacher_logits, code, student_head)
-    return small[1, 0, 0], small[0, :, 3], hidden_grad, head_grad
+    )(
+        hidden, teacher_logits, sampled_ids.reshape(1, RB), loss_mask.reshape(1, RB), student_head
+    )
+    loss, ratio, hidden_grad, head_grad = pl.pallas_call(
+        store_all,
+        out_shape=tuple(jax.ShapeDtypeStruct(shape, kind) for shape, kind in shapes),
+        in_specs=[vmem] * 4,
+        out_specs=(any_space,) * 4,
+        scratch_shapes=[DMA((4,))],
+        compiler_params=pltpu.CompilerParams(vmem_limit_bytes=1024 * 1024),
+    )(*[pltpu.with_memory_space_constraint(part, pltpu.VMEM) for part in kept])
+    return loss[0, 0], ratio[0], hidden_grad, head_grad
 
 
 def solution(mesh):

time: 64.5 us -> 59.7 us (0.926)
  local copies, waits for them, and re-layouts: 9.43 us -> 0 us
  Pallas kernels: 53.4 us -> 58.9 us
  other arithmetic: 0.68 us -> 0 us
    unnamed x2 -> x0, local copies, waits for them, and re-layouts: 6.28 us -> none
    pallas_call x1 -> x2, Pallas kernels: 53.4 us -> 58.9 us  [the longest x1 56.1 us: per_device(): pl.pallas_call(functools.partial(kernel, T, V, WA, WB, NCH), out_shape=tu...]
    slice x2 -> x0, local copies, waits for them, and re-layouts: 2.56 us -> none  [per_device(): return (small[1, 0, 0], small[0, :, 3], hidden_grad, head_grad)]
    convert_element_type x1 -> x0, other arithmetic: 0.68 us -> none  [per_device(): jnp.stack([sampled_ids, loss_mask]).astype(F32)]
where the time goes in v2:
time: 59.7 us; the launch traced here: 59.5 us
  Pallas kernels  58.9 us (99%)
  between operations  0.64 us (1%)
    pallas_call x1, Pallas kernels, per_device(): pl.pallas_call(functools.partial(kernel, T, V, WA, WB, NCH), out_shape=tu...  56.1 us
    pallas_call x1, Pallas kernels, per_device(): pl.pallas_call(store_all, out_shape=tuple((jax.ShapeDtypeStruct(shape, ki...  2.82 us

profile of v2, /device:TPU:0, one launch (start us, length us, event | category | flops | bytes accessed | tf_op | source)
XLA Modules:
  0.0 59.5 jit_solution(2024296763675507134)
XLA Ops:
  0.6 56.1 %shard_map.84 = (f32[1,1]{1,0:T(1,128)}, f32[1,8]{1,0:T(1,128)S(1)}, bf16[8,3584]{1,0:T(8,128)(2,1)S(1)}, bf16[3584,640]{1,0:T(8,128)(2,1)S(1)}) custom-call(bf16[32,3584]{1,0:T(8,128)(2,1)} %hidden.1, bf16[256,640]{1,0:T(8,128)(2,1)} %teacher_hbm.1, s32[1,32]{1,0:T(1,128)} %bitcast.4, s32[1,32]{1,0:T(1,128)} %bitcast.5, bf16[3584,640]{1,0:T(8,128)(2,1)} %head_hbm.1), custom_call_target="tpu_custom_call" | custom-call | tf_op jit(solution)/shard_map/pallas_call | solution.py:380
  56.7 2.8 %shard_map.85 = (f32[1,1]{1,0:T(1,128)}, f32[1,8]{1,0:T(1,128)}, bf16[8,3584]{1,0:T(8,128)(2,1)}, bf16[3584,640]{1,0:T(8,128)(2,1)}) custom-call(f32[1,1]{1,0:T(1,128)} %get-tuple-element.12.a, f32[1,8]{1,0:T(1,128)S(1)} %get-tuple-element.13.b, bf16[8,3584]{1,0:T(8,128)(2,1)S(1)} %get-tuple-element.14.c, bf16[3584,640]{1,0:T(8,128)(2,1)S(1)} %get-tuple-element.15.d), custom_call_target="tpu_custom_call" | custom-call | tf_op jit(solution)/shard_map/pallas_call | solution.py:425

commit v3 on v2

--- a/solution.py
+++ b/solution.py
@@ -329,7 +329,7 @@
                 other_z(k),
             )
 
-    lag = 4 if NCH > 4 else 2
+    lag = NCH - 1
     for i in range(NCH + lag):
         if i < NCH:
             second(turns[i])
@@ -368,7 +368,7 @@
     a = (units * 5) // 28
     b = (units - V * a) // 2
     WA, WB = a * 128, b * 128
-    NCH = D // 256 if (D // 256) % 2 == 0 else 2
+    NCH = 4
     CW = D // NCH
     DMA = pltpu.SemaphoreType.DMA
     H = R // 8

time: 59.7 us -> 54.6 us (0.915)
  Pallas kernels: 58.9 us -> 53.8 us
    pallas_call x1, Pallas kernels: 56.1 us -> 51 us  [per_device(): pl.pallas_call(functools.partial(kernel, T, V, WA, WB, NCH), out_shape=tu...]
where the time goes in v3:
time: 54.6 us; the launch traced here: 54.5 us
  Pallas kernels  53.8 us (99%)
  between operations  0.64 us (1%)
    pallas_call x1, Pallas kernels, per_device(): pl.pallas_call(functools.partial(kernel, T, V, WA, WB, NCH), out_shape=tu...  51 us
    pallas_call x1, Pallas kernels, per_device(): pl.pallas_call(store_all, out_shape=tuple((jax.ShapeDtypeStruct(shape, ki...  2.82 us

profile of v3, /device:TPU:0, one launch (start us, length us, event | category | flops | bytes accessed | tf_op | source)
XLA Modules:
  0.0 54.5 jit_solution(11616246077082884651)
XLA Ops:
  0.6 51.0 %shard_map.84 = (f32[1,1]{1,0:T(1,128)}, f32[1,8]{1,0:T(1,128)S(1)}, bf16[8,3584]{1,0:T(8,128)(2,1)S(1)}, bf16[3584,640]{1,0:T(8,128)(2,1)S(1)}) custom-call(bf16[32,3584]{1,0:T(8,128)(2,1)} %hidden.1, bf16[256,640]{1,0:T(8,128)(2,1)} %teacher_hbm.1, s32[1,32]{1,0:T(1,128)} %bitcast.4, s32[1,32]{1,0:T(1,128)} %bitcast.5, bf16[3584,640]{1,0:T(8,128)(2,1)} %head_hbm.1), custom_call_target="tpu_custom_call" | custom-call | tf_op jit(solution)/shard_map/pallas_call | solution.py:380
  51.7 2.8 %shard_map.85 = (f32[1,1]{1,0:T(1,128)}, f32[1,8]{1,0:T(1,128)}, bf16[8,3584]{1,0:T(8,128)(2,1)}, bf16[3584,640]{1,0:T(8,128)(2,1)}) custom-call(f32[1,1]{1,0:T(1,128)} %get-tuple-element.12.a, f32[1,8]{1,0:T(1,128)S(1)} %get-tuple-element.13.b, bf16[8,3584]{1,0:T(8,128)(2,1)S(1)} %get-tuple-element.14.c, bf16[3584,640]{1,0:T(8,128)(2,1)S(1)} %get-tuple-element.15.d), custom_call_target="tpu_custom_call" | custom-call | tf_op jit(solution)/shard_map/pallas_call | solution.py:425
